TPU v7x, 256 devices: a whole 4x4x8 slice. The times are simulated.
256 devices in a mesh: seq: 4 (over x_hi, core), ctx: 8 (over z), head: 8 (over x_lo, y).
Axes of the slice: x: 4 (x_hi: 2, x_lo: 2; x = x_hi * 2 + x_lo), y: 4, z: 8, core: 2. Of those that a mesh axis runs over, the one named last changes fastest.
Arguments:
- stream: bfloat16 [4, 512, 2880], P('seq', 'ctx'), may hold values from -6 to 6
- query_weight: bfloat16 [2880, 4096], P(None, 'head'), may hold values from -0.109375 to 0.109375
- cache_keys: bfloat16 [4, 16384, 8, 64], P('seq', 'ctx', 'head'), may hold values from -1000 to 1000
- cache_values: bfloat16 [4, 16384, 8, 64], P('seq', 'ctx', 'head'), may hold values from -6 to 6
- new_keys: bfloat16 [4, 512, 8, 64], P('seq', 'ctx', 'head'), may hold values from -18 to 18
- new_values: bfloat16 [4, 512, 8, 64], P('seq', 'ctx', 'head'), may hold values from -6 to 6
- out_weight: bfloat16 [4096, 2880], P('head'), may hold values from -0.09375 to 0.09375
- norm_gain: float32 [2880], replicated, may hold values from 0.5 to 1.5
- expert_ids: int32 [4, 512, 4], P('seq', 'ctx'), may hold values from 0 to 31, all different within a row; in each aligned block of 64 rows (0 to 63, 64 to 127, ..., all dimensions but the last counted through in order) at most 16 rows name the same one
- expert_weights: float32 [4, 512, 4], P('seq', 'ctx'), may hold values from 0.1 to 1
- gate_weight: bfloat16 [32, 2880, 2880], P(('seq', 'ctx'), None, 'head'), may hold values from -0.109375 to 0.109375
- up_weight: bfloat16 [32, 2880, 2880], P(('seq', 'ctx'), None, 'head'), may hold values from -0.109375 to 0.109375
- down_weight: bfloat16 [32, 2880, 2880], P(('seq', 'ctx'), 'head'), may hold values from -0.109375 to 0.109375
Outputs:
- mixed: bfloat16 [4, 512, 2880], P('seq', 'ctx', 'head')
Inputs may be any that keep to these rules, and one draw needn't show every extreme that they name: `expert_ids`: in each aligned block of 64 rows (the tokens of one device) no expert is named by more than 16 rows; each row names 4 different experts.
All inputs are finite; a program needn't handle non-finite values.
Results may differ from a plain program's by a relative error of at most 0.015.
Values may be sent and summed in bfloat16 or wider, within the bound.
A program may use at most 64 MiB of HBM per device.

v0:
```python
import math
import jax
import jax.numpy as jnp
from jax import lax
from jax.sharding import PartitionSpec as P

CAP = 16


def sent_to_all(array, axis):
    copies = jnp.broadcast_to(array, (lax.axis_size(axis), *array.shape))
    return lax.all_to_all(copies, axis, split_axis=0, concat_axis=0, tiled=True)


def joined_along(tiles, dim):
    shape = list(tiles.shape[1:])
    shape[dim] *= tiles.shape[0]
    return jnp.moveaxis(tiles, 0, dim).reshape(shape)


def gathered_copies(array, axis, dim):
    tiles = sent_to_all(array, axis)
    return joined_along(tiles, dim)


def split_up(array, dim, count):
    before, after = (array.shape[:dim], array.shape[dim + 1 :])
    return jnp.moveaxis(array.reshape(*before, count, -1, *after), dim, 0)


def sent_and_summed(array, axis, dim):
    tiles = split_up(array, dim, lax.axis_size(axis))
    arrived = lax.all_to_all(tiles, axis, split_axis=0, concat_axis=0, tiled=True)
    return arrived.astype(jnp.float32).sum(axis=0)


def taken_together(array, axis):
    return sent_to_all(array, axis).sum(axis=0)


def body(
    stream,
    query_weight,
    cache_keys,
    cache_values,
    new_keys,
    new_values,
    out_weight,
    norm_gain,
    expert_ids,
    expert_weights,
    gate_weight,
    up_weight,
    down_weight,
):
    tokens = stream[0]
    count = tokens.shape[0]
    model = tokens.shape[1]
    kv_local = cache_keys.shape[2]
    head_dim = cache_keys.shape[3]
    group = query_weight.shape[1] // (kv_local * head_dim)
    cache_len = cache_keys.shape[1]
    height = count * group
    cycles = lax.axis_size("ctx")
    place = lax.axis_index("ctx")
    scale = 1.0 / math.sqrt(head_dim)
    query = jnp.dot(tokens, query_weight, preferred_element_type=jnp.float32).astype(jnp.bfloat16)
    query = (
        query.reshape(count, kv_local, group, head_dim)
        .transpose(1, 0, 2, 3)
        .reshape(kv_local, height, head_dim)
    )
    keys = jnp.concatenate([cache_keys[0], new_keys[0]], axis=0).transpose(1, 0, 2)
    values = jnp.concatenate([cache_values[0], new_values[0]], axis=0).transpose(1, 0, 2)
    extent = keys.shape[1]
    key_index = lax.broadcasted_iota(jnp.int32, (height, extent), 1)
    tok_index = lax.broadcasted_iota(jnp.int32, (height, extent), 0) // group
    fresh = key_index - cache_len
    blank = (
        jnp.full((kv_local, height), -jnp.inf, jnp.float32),
        jnp.zeros((kv_local, height), jnp.float32),
        jnp.zeros((kv_local, height, head_dim), jnp.float32),
    )

    def absorb(block, state, sources):
        top, total, numerator = state
        anchor = sources[:, None]
        allowed = (
            (key_index < cache_len) | (place < anchor) | (place == anchor) & (fresh <= tok_index)
        )
        scores = jnp.einsum("hrd,hkd->hrk", block, keys, preferred_element_type=jnp.float32) * scale
        scores = jnp.where(allowed[None], scores, -jnp.inf)
        new_top = jnp.max(scores, axis=-1)
        weights = jnp.exp(scores - new_top[..., None])
        fade = jnp.exp(top - new_top)
        total = total * fade + jnp.sum(weights, axis=-1)
        numerator = numerator * fade[..., None] + jnp.einsum(
            "hrk,hkd->hrd", weights.astype(jnp.bfloat16), values, preferred_element_type=jnp.float32
        )
        return (new_top, total, numerator)

    everyone = gathered_copies(query[None], "ctx", 0)

    def partial_state(operands):
        block, source = operands
        return absorb(block, blank, jnp.full((height,), source, jnp.int32))

    pieces = lax.map(partial_state, (everyone, lax.iota(jnp.int32, cycles)))
    tops, totals, numerators = lax.all_to_all(
        pieces, "ctx", split_axis=0, concat_axis=0, tiled=True
    )
    top = jnp.max(tops, axis=0)
    fade = jnp.exp(tops - top[None])
    total = jnp.sum(totals * fade, axis=0)
    numerator = jnp.sum(numerators * fade[..., None], axis=0)
    attn = (numerator / total[..., None]).astype(jnp.bfloat16)
    attn = (
        attn.reshape(kv_local, count, group, head_dim)
        .transpose(1, 0, 2, 3)
        .reshape(count, kv_local * group * head_dim)
    )
    projected = jnp.dot(attn, out_weight, preferred_element_type=jnp.float32)
    width = model // lax.axis_size("head")
    offset = lax.axis_index("head") * width
    resid_own = lax.dynamic_slice_in_dim(tokens, offset, width, 1).astype(
        jnp.float32
    ) + sent_and_summed(projected.astype(jnp.bfloat16), "head", 1)
    power = taken_together(jnp.sum(resid_own * resid_own, axis=-1), "head")
    gain_own = lax.dynamic_slice_in_dim(norm_gain, offset, width, 0)
    normed = (resid_own * lax.rsqrt(power[:, None] / model + 1e-05) * gain_own).astype(jnp.bfloat16)
    experts = lax.axis_size("seq") * lax.axis_size("ctx")
    slots = experts * CAP
    chosen = expert_ids[0].reshape(-1)
    onehot = (chosen[:, None] == lax.broadcasted_iota(jnp.int32, (1, experts), 1)).astype(jnp.int32)
    before = jnp.cumsum(onehot, axis=0) - onehot
    target = chosen * CAP + jnp.sum(before * onehot, axis=1)
    matches = target[None, :] == lax.broadcasted_iota(jnp.int32, (slots, 1), 0)
    select = jnp.sum(matches.astype(jnp.float32).reshape(slots, count, -1), axis=-1).astype(
        jnp.bfloat16
    )
    packed = jnp.dot(select, normed, preferred_element_type=jnp.float32).astype(jnp.bfloat16)
    packed = packed.reshape(experts, CAP, normed.shape[1])
    arrived = lax.all_to_all(packed, ("seq", "ctx"), split_axis=0, concat_axis=0, tiled=True)
    rows = arrived.reshape(slots, normed.shape[1])
    piece = lax.all_gather(rows, "head", axis=1, tiled=True)
    gate_rows = gate_weight[0]
    up_rows = up_weight[0]
    gate = jnp.dot(piece, gate_rows, preferred_element_type=jnp.float32)
    up = jnp.dot(piece, up_rows, preferred_element_type=jnp.float32)
    hidden = (gate * jax.nn.sigmoid(1.702 * gate) * (up + 1.0)).astype(jnp.bfloat16)
    columns = down_weight[0]
    expert_out = sent_and_summed(
        jnp.einsum("fd,rf->dr", columns, hidden, preferred_element_type=jnp.float32).astype(
            jnp.bfloat16
        ),
        "head",
        0,
    ).astype(jnp.bfloat16)
    returned = lax.all_to_all(expert_out, ("seq", "ctx"), split_axis=1, concat_axis=1, tiled=True)
    spread_weights = jnp.where(matches.T, expert_weights[0].reshape(-1)[:, None], 0.0)
    spread_weights = jnp.sum(spread_weights.reshape(count, -1, slots), axis=1)
    moe = lax.dot_general(
        spread_weights,
        returned.astype(jnp.float32),
        (((1,), (1,)), ((), ())),
        precision=lax.Precision.HIGHEST,
    )
    return (resid_own + moe).astype(jnp.bfloat16)[None]


def solution(mesh):
    in_specs = (
        P("seq", "ctx", None),
        P(None, "head"),
        P("seq", "ctx", "head", None),
        P("seq", "ctx", "head", None),
        P("seq", "ctx", "head", None),
        P("seq", "ctx", "head", None),
        P("head", None),
        P(),
        P("seq", "ctx", None),
        P("seq", "ctx", None),
        P(("seq", "ctx"), None, "head"),
        P(("seq", "ctx"), None, "head"),
        P(("seq", "ctx"), "head", None),
    )
    out_specs = P("seq", "ctx", "head")
    return jax.shard_map(body, mesh=mesh, in_specs=in_specs, out_specs=out_specs, check_vma=False)
```

profile of v0, /device:TPU:1, one launch (start us, length us, event | category | flops | bytes accessed | tf_op | source)
XLA Modules:
  0.0 326.2 jit_solution(1258331897230026775)
XLA Ops:
  6.5 2.7 convolution_convert_fusion.3
  10.4 9.0 %all-to-all-start = ((bf16[8,1,1,512,64]{3,4,2,1,0:T(8,128)(2,1)}), bf16[8,1,1,512,64]{3,4,2,1,0:T(8,128)(2,1)}, u32[]{:S(2)}, u32[]{:S(2)}) async-start(bf16[8,1,1,512,64]{3,4,2,1,0:T(8,128)(2,1)} %broadcast_in_dim.65), calls=%async_computation | async-start | bytes 1048576 | tf_op jit(solution)/shard_map/all_to_all | solution.py:12
  19.4 1.0 copy.57
  20.4 1.9 copy.58
  24.1 2.2 maximum_bitcast_fusion
  26.4 11.1 %all-to-all-done = bf16[8,1,1,512,64]{3,4,2,1,0:T(8,128)(2,1)} async-done(((bf16[8,1,1,512,64]{3,4,2,1,0:T(8,128)(2,1)}), bf16[8,1,1,512,64]{3,4,2,1,0:T(8,128)(2,1)}, u32[]{:S(2)}, u32[]{:S(2)}) %all-to-all-start) | async-done | bytes 524320 | tf_op jit(solution)/shard_map/all_to_all | solution.py:12
  37.4 55.5 %while.17 = (s32[]{:T(128)}, f32[8,1,512]{2,1,0:T(1,128)S(1)}, f32[8,1,512]{2,1,0:T(1,128)S(1)}, f32[8,1,512,64]{2,3,1,0:T(8,128)}, s32[8]{0:T(128)S(1)}, /*inde...) while((s32[]{:T(128)}, f32[8,1,512]{2,1,0:T(1,128)S(1)}, ...), condition=%wide.region_3.4_spmd.clone, body=%wide.region_0.3_spmd.clone.sunk | while | flops 290915840 | bytes 14024361 | solution.py:108
  39.3 3.0 fusion.82
  42.3 1.4 fusion.84
  46.2 3.0 fusion.82
  49.2 1.4 fusion.84
  53.1 3.0 fusion.82
  56.1 1.4 fusion.84
  60.1 3.0 fusion.82
  63.1 1.4 fusion.84
  67.0 3.0 fusion.82
  70.0 1.4 fusion.84
  73.9 3.0 fusion.82
  77.0 1.4 fusion.84
  80.9 3.0 fusion.82
  83.9 1.4 fusion.84
  87.8 3.0 fusion.82
  90.8 1.4 fusion.84
  92.9 9.0 %all_to_all.53 = f32[8,1,512]{2,1,0:T(1,128)S(1)} all-to-all(f32[8,1,512]{2,1,0:T(1,128)S(1)} %get-tuple-element.143), channel_id=1, replica_groups=mesh['seq'=4,'ctx'=8,'head'=8] {'ctx'}, dimensions={0} | all-to-all | bytes 32768 | tf_op jit(solution)/shard_map/all_to_all | solution.py:109
  102.0 9.0 %all_to_all.54 = f32[8,1,512]{2,1,0:T(1,128)S(1)} all-to-all(f32[8,1,512]{2,1,0:T(1,128)S(1)} %get-tuple-element.144), channel_id=1, replica_groups=mesh['seq'=4,'ctx'=8,'head'=8] {'ctx'}, dimensions={0} | all-to-all | bytes 32768 | tf_op jit(solution)/shard_map/all_to_all | solution.py:109
  110.9 4.2 %all-to-all-start.1 = ((f32[8,1,512,64]{2,3,1,0:T(8,128)}), f32[8,1,512,64]{2,3,1,0:T(8,128)}, u32[]{:S(2)}, u32[]{:S(2)}) async-start(f32[8,1,512,64]{2,3,1,0:T(8,128)} %get-tuple-element.142), calls=%async_computation.1 | async-start | bytes 2097152 | tf_op jit(solution)/shard_map/all_to_all | solution.py:109
  117.8 24.6 %all-to-all-done.1 = f32[8,1,512,64]{2,3,1,0:T(8,128)} async-done(((f32[8,1,512,64]{2,3,1,0:T(8,128)}), f32[8,1,512,64]{2,3,1,0:T(8,128)}, u32[]{:S(2)}, u32[]{:S(2)}) %all-to-all-start.1) | async-done | bytes 1048608 | tf_op jit(solution)/shard_map/all_to_all | solution.py:109
  142.4 1.4 multiply_reduce_fusion
  144.1 1.7 convolution_convert_fusion.1
  145.8 1.5 reshape.190
  148.1 5.1 %all-to-all-start.4 = ((bf16[8,64,360]{2,1,0:T(8,128)(2,1)}), bf16[8,64,360]{2,1,0:T(8,128)(2,1)S(1)}, u32[]{:S(2)}, u32[]{:S(2)}) async-start(bf16[8,64,360]{2,1,0:T(8,128)(2,1)} %bitcast.105), calls=%async_computation.4 | async-start | bytes 786432 | tf_op jit(solution)/shard_map/all_to_all | solution.py:33
  153.6 6.3 %all-to-all-done.4 = bf16[8,64,360]{2,1,0:T(8,128)(2,1)S(1)} async-done(((bf16[8,64,360]{2,1,0:T(8,128)(2,1)}), bf16[8,64,360]{2,1,0:T(8,128)(2,1)S(1)}, u32[]{:S(2)}, u32[]{:S(2)}) %all-to-all-start.4) | async-done | bytes 368672 | tf_op jit(solution)/shard_map/all_to_all | solution.py:33
  159.9 1.0 multiply_reduce_fusion.1
  161.6 3.3 %all-to-all-start.5 = ((f32[8,1,64]{2,1,0:T(1,128)}), f32[8,1,64]{2,1,0:T(1,128)S(1)}, u32[]{:S(2)}, u32[]{:S(2)}) async-start(f32[8,1,64]{2,1,0:T(1,128)} %broadcast_in_dim.69), calls=%async_computation.5 | async-start | bytes 8192 | tf_op jit(solution)/shard_map/all_to_all | solution.py:12
  165.8 3.9 %all-to-all-done.5 = f32[8,1,64]{2,1,0:T(1,128)S(1)} async-done(((f32[8,1,64]{2,1,0:T(1,128)}), f32[8,1,64]{2,1,0:T(1,128)S(1)}, u32[]{:S(2)}, u32[]{:S(2)}) %all-to-all-start.5) | async-done | bytes 2080 | tf_op jit(solution)/shard_map/all_to_all | solution.py:12
  169.8 2.0 convolution_convert_fusion.2
  171.8 1.2 copy.69
  173.0 23.9 %all_to_all.55 = bf16[32,16,360]{2,1,0:T(8,128)(2,1)} all-to-all(bf16[32,16,360]{2,1,0:T(8,128)(2,1)S(1)} %bitcast.126), channel_id=1, replica_groups=mesh['seq'=4,'ctx'=8,'head'=8] {'seq','ctx'}, dimensions={0} | all-to-all | bytes 737280 | tf_op jit(solution)/shard_map/all_to_all | solution.py:143
  196.9 1.9 copy.70
  198.8 36.6 %all-gather.2.cloned.1.call-done = bf16[512,2880]{0,1:T(8,128)(2,1)} async-done(((bf16[512,360]{0,1:T(8,128)(2,1)}), bf16[512,2880]{0,1:T(8,128)(2,1)}) %all-gather.2.cloned.1.call-update) | async-done | bytes 2949136 | tf_op jit(solution)/shard_map/all_gather | solution.py:145
  235.5 4.7 %fusion.30 = f32[512,360]{0,1:T(8,128)} fusion(bf16[512,2880]{0,1:T(8,128)(2,1)} %all-gather.2.cloned.1.call-done, bf16[1,2880,360]{1,2,0:T(8,128)(2,1)} %param.25), kind=kOutput, calls=%fused_computation.30 | convolution fusion | flops 1061683200 | bytes 5760000 | tf_op jit(solution)/shard_map/dot_general | solution.py:148
  240.1 7.9 %convolution_convert_fusion = bf16[512,2880]{0,1:T(8,128)(2,1)} fusion(bf16[1,360,2880]{2,1,0:T(8,128)(2,1)} %param.27, bf16[512,2880]{0,1:T(8,128)(2,1)} %all-gather.2.cloned.1.call-done, bf16[1,2880,360]{1,2,0:T(8,128)(2,1)} %param.26, f32[512,360]{0,1:T(8,128)} %fusion.30), kind=kOutput, calls=%fused_computation.25 | convolution fusion | flops 2126315520 | bytes 10782720 | tf_op jit(solution)/shard_map/fd,rf->dr/dot_general | solution.py:153
  248.1 37.1 %all_to_all.56 = bf16[8,360,512]{2,1,0:T(8,128)(2,1)} all-to-all(bf16[8,360,512]{2,1,0:T(8,128)(2,1)} %bitcast.121), channel_id=1, replica_groups=mesh['seq'=4,'ctx'=8,'head'=8] {'head'}, dimensions={0} | all-to-all | bytes 5898240 | tf_op jit(solution)/shard_map/all_to_all | solution.py:33
  285.2 2.4 reduce_sum.109
  287.6 0.9 copy.71
  288.5 14.1 %all-to-all-start.8 = ((bf16[360,32,16]{0,2,1:T(8,128)(2,1)}), bf16[360,32,16]{0,2,1:T(8,128)(2,1)S(1)}, u32[]{:S(2)}, u32[]{:S(2)}) async-start(bf16[360,32,16]{0,2,1:T(8,128)(2,1)} %bitcast.125), calls=%async_computation.8 | async-start | bytes 786432 | tf_op jit(solution)/shard_map/all_to_all | solution.py:159
  303.4 14.1 %all-to-all-done.8 = bf16[360,32,16]{0,2,1:T(8,128)(2,1)S(1)} async-done(((bf16[360,32,16]{0,2,1:T(8,128)(2,1)}), bf16[360,32,16]{0,2,1:T(8,128)(2,1)S(1)}, u32[]{:S(2)}, u32[]{:S(2)}) %all-to-all-start.8) | async-done | bytes 368672 | tf_op jit(solution)/shard_map/all_to_all | solution.py:159
  317.5 1.8 fusion.42
  (88 shorter events, 19.6 us)
Async XLA Ops:
  6.5 137.5 %copy-start = (bf16[512,2880]{0,1:T(8,128)(2,1)S(1)}, bf16[512,2880]{0,1:T(8,128)(2,1)}, u32[]{:S(2)}) copy-start(bf16[512,2880]{0,1:T(8,128)(2,1)} %param.21) | copy-start | bytes 8847364
  6.5 12.8 %copy-start.1 = (bf16[1,2048,1,64]{1,3,2,0:T(8,128)(2,1)S(1)}, bf16[1,2048,1,64]{1,3,2,0:T(8,128)(2,1)}, u32[]{:S(2)}) copy-start(bf16[1,2048,1,64]{1,3,2,0:T(8,128)(2,1)} %param.17) | copy-start | bytes 786436
  6.5 17.6 %copy-start.2 = (bf16[1,64,1,64]{3,1,2,0:T(8,128)(2,1)S(1)}, bf16[1,64,1,64]{3,1,2,0:T(8,128)(2,1)}, u32[]{:S(2)}) copy-start(bf16[1,64,1,64]{3,1,2,0:T(8,128)(2,1)} %param.19) | copy-start | bytes 24580
  6.5 17.6 %copy-start.3 = (bf16[1,64,1,64]{3,1,2,0:T(8,128)(2,1)S(1)}, bf16[1,64,1,64]{3,1,2,0:T(8,128)(2,1)}, u32[]{:S(2)}) copy-start(bf16[1,64,1,64]{3,1,2,0:T(8,128)(2,1)} %param.20) | copy-start | bytes 24580
  10.4 27.1 %all-to-all-start = ((bf16[8,1,1,512,64]{3,4,2,1,0:T(8,128)(2,1)}), bf16[8,1,1,512,64]{3,4,2,1,0:T(8,128)(2,1)}, u32[]{:S(2)}, u32[]{:S(2)}) async-start(bf16[8,1,1,512,64]{3,4,2,1,0:T(8,128)(2,1)} %broadcast_in_dim.65), calls=%async_computation | async-start | bytes 1048576 | tf_op jit(solution)/shard_map/all_to_all | solution.py:12
  37.4 77.7 %copy-start.7 = (s32[1,64,4]{1,2,0:T(4,128)S(1)}, s32[1,64,4]{1,2,0:T(4,128)}, u32[]{:S(2)}) copy-start(s32[1,64,4]{1,2,0:T(4,128)} %param.23) | copy-start | bytes 3076
  110.9 31.5 %all-to-all-start.1 = ((f32[8,1,512,64]{2,3,1,0:T(8,128)}), f32[8,1,512,64]{2,3,1,0:T(8,128)}, u32[]{:S(2)}, u32[]{:S(2)}) async-start(f32[8,1,512,64]{2,3,1,0:T(8,128)} %get-tuple-element.142), calls=%async_computation.1 | async-start | bytes 2097152 | tf_op jit(solution)/shard_map/all_to_all | solution.py:109
  116.9 0.6 copy-start.4
  144.1 9.2 %slice-start = ((s32[32,3]{0,1:T(4,128)}), s32[32,2]{0,1:T(2,128)S(1)}, s32[]{:S(2)}) async-start(s32[32,3]{0,1:T(4,128)} %copy-done.4), calls=%async_computation.10 | async-start | bytes 2048 | tf_op jit(solution)/shard_map/slice.1
  144.1 9.2 %copy-start.5 = (s32[256]{0:T(256)S(1)}, s32[256]{0:T(256)}, u32[]{:S(2)}) copy-start(s32[256]{0:T(256)} %eq.54) | copy-start | bytes 3076
  148.1 11.7 %all-to-all-start.4 = ((bf16[8,64,360]{2,1,0:T(8,128)(2,1)}), bf16[8,64,360]{2,1,0:T(8,128)(2,1)S(1)}, u32[]{:S(2)}, u32[]{:S(2)}) async-start(bf16[8,64,360]{2,1,0:T(8,128)(2,1)} %bitcast.105), calls=%async_computation.4 | async-start | bytes 786432 | tf_op jit(solution)/shard_map/all_to_all | solution.py:33
  161.6 8.2 %all-to-all-start.5 = ((f32[8,1,64]{2,1,0:T(1,128)}), f32[8,1,64]{2,1,0:T(1,128)S(1)}, u32[]{:S(2)}, u32[]{:S(2)}) async-start(f32[8,1,64]{2,1,0:T(1,128)} %broadcast_in_dim.69), calls=%async_computation.5 | async-start | bytes 8192 | tf_op jit(solution)/shard_map/all_to_all | solution.py:12
  164.9 70.6 %all-gather.2.cloned.1.call-start = ((), (), s32[]{:S(2)}) async-start(), calls=%async_computation.9 | async-start | bytes 3317760 | tf_op jit(solution)/shard_map/all_gather | solution.py:145
  285.2 17.4 %copy-start.6 = (f32[1,64,4]{1,2,0:T(4,128)S(1)}, f32[1,64,4]{1,2,0:T(4,128)}, u32[]{:S(2)}) copy-start(f32[1,64,4]{1,2,0:T(4,128)} %param.24) | copy-start | bytes 3076
  288.5 29.0 %all-to-all-start.8 = ((bf16[360,32,16]{0,2,1:T(8,128)(2,1)}), bf16[360,32,16]{0,2,1:T(8,128)(2,1)S(1)}, u32[]{:S(2)}, u32[]{:S(2)}) async-start(bf16[360,32,16]{0,2,1:T(8,128)(2,1)} %bitcast.125), calls=%async_computation.8 | async-start | bytes 786432 | tf_op jit(solution)/shard_map/all_to_all | solution.py:159
Sparse Core Ops, SparseCore 0:
  198.9 36.4 all-gather.1
where the time goes:
time: 328 us; the launch traced here: 326 us
  waiting for transfers between devices  96.7 us (29%)
  blocking collectives  79.1 us (24%)
  matrix products  56.1 us (17%)
  starting transfers between devices  35.8 us (11%)
  local copies, waits for them, and re-layouts  19 us (6%)
  other arithmetic  16 us (5%)
  between operations  13.6 us (4%)
  loops' own time  9.98 us (3%)
    all_to_all x1, blocking collectives, sent_and_summed(): lax.all_to_all(tiles, axis, split_axis=0, concat_axis=0, tiled=True)  37.1 us
    all_gather x1, waiting for transfers between devices, body(): piece = lax.all_gather(rows, 'head', axis=1, tiled=True)  36.6 us
    all_to_all x1, waiting for transfers between devices, body(): lax.all_to_all(pieces, 'ctx', split_axis=0, concat_axis=0, tiled=True)  24.6 us
    dot_general x8, matrix products, absorb(): jnp.einsum('hrd,hkd->hrk', block, keys, preferred_element_type=jnp.float32)  24 us
    all_to_all x1, blocking collectives, body(): lax.all_to_all(packed, ('seq', 'ctx'), split_axis=0, concat_axis=0, tiled...  23.9 us
    all_to_all x2, blocking collectives, body(): lax.all_to_all(pieces, 'ctx', split_axis=0, concat_axis=0, tiled=True)  18 us
    all_to_all x2, waiting for transfers between devices, sent_to_all(): return lax.all_to_all(copies, axis, split_axis=0, concat_axis=0, tiled=True)  15 us
    all_to_all x1, waiting for transfers between devices, body(): lax.all_to_all(expert_out, ('seq', 'ctx'), split_axis=1, concat_axis=1, t...  14.1 us
  transfers between devices with their start and end apart: 6, of which 6 were waited for; matrix products, arithmetic and copies ran while one was open for 3% of the time, Pallas kernels for 0%

commit v1 on v0

--- a/solution.py
+++ b/solution.py
@@ -142,7 +142,8 @@
     packed = packed.reshape(experts, CAP, normed.shape[1])
     arrived = lax.all_to_all(packed, ("seq", "ctx"), split_axis=0, concat_axis=0, tiled=True)
     rows = arrived.reshape(slots, normed.shape[1])
-    piece = lax.all_gather(rows, "head", axis=1, tiled=True)
+    outgoing = jnp.stack([rows] * lax.axis_size("head"))
+    piece = jnp.concatenate(lax.all_to_all(outgoing, "head", 0, 0), axis=1)
     gate_rows = gate_weight[0]
     up_rows = up_weight[0]
     gate = jnp.dot(piece, gate_rows, preferred_element_type=jnp.float32)

time: 328 us -> 309 us (0.942)
  blocking collectives: 79.1 us -> 119 us
  waiting for transfers between devices: 96.7 us -> 59.3 us
  between operations: 13.6 us -> 0.24 us
  starting transfers between devices: 35.8 us -> 28.9 us
    all_to_all x0 -> x1, blocking collectives: none -> 38.2 us  [body(): piece = jnp.concatenate(lax.all_to_all(outgoing, 'head', 0, 0), axis=1)]
    all_gather x1 -> x0, waiting for transfers between devices: 36.6 us -> none  [body(): piece = lax.all_gather(rows, 'head', axis=1, tiled=True)]
    all_to_all x1, starting transfers between devices: 14.1 us -> 7.28 us  [body(): lax.all_to_all(expert_out, ('seq', 'ctx'), split_axis=1, concat_axis=1, t...]
  transfers between devices with their start and end apart: 6 -> 5, of which waited for: 6 -> 5; matrix products, arithmetic and copies ran while one was open for 3% -> 4% of each run, Pallas kernels for 0% -> 0%
where the time goes in v1:
time: 309 us; the launch traced here: 308 us
  blocking collectives  119 us (39%)
  waiting for transfers between devices  59.3 us (19%)
  matrix products  53.6 us (17%)
  starting transfers between devices  28.9 us (9%)
  local copies, waits for them, and re-layouts  20.8 us (7%)
  other arithmetic  16 us (5%)
  loops' own time  9.98 us (3%)
    all_to_all x1, blocking collectives, sent_and_summed(): lax.all_to_all(tiles, axis, split_axis=0, concat_axis=0, tiled=True)  38.8 us
    all_to_all x1, blocking collectives, body(): piece = jnp.concatenate(lax.all_to_all(outgoing, 'head', 0, 0), axis=1)  38.2 us
    all_to_all x1, blocking collectives, body(): lax.all_to_all(packed, ('seq', 'ctx'), split_axis=0, concat_axis=0, tiled...  24.1 us
    dot_general x8, matrix products, absorb(): jnp.einsum('hrd,hkd->hrk', block, keys, preferred_element_type=jnp.float32)  24 us
    all_to_all x1, waiting for transfers between devices, body(): lax.all_to_all(pieces, 'ctx', split_axis=0, concat_axis=0, tiled=True)  23.9 us
    all_to_all x2, blocking collectives, body(): lax.all_to_all(pieces, 'ctx', split_axis=0, concat_axis=0, tiled=True)  18 us
    all_to_all x2, waiting for transfers between devices, sent_to_all(): return lax.all_to_all(copies, axis, split_axis=0, concat_axis=0, tiled=True)  15 us
    all_to_all x1, waiting for transfers between devices, body(): lax.all_to_all(expert_out, ('seq', 'ctx'), split_axis=1, concat_axis=1, t...  14.1 us
  transfers between devices with their start and end apart: 5, of which 5 were waited for; matrix products, arithmetic and copies ran while one was open for 4% of the time, Pallas kernels for 0%

profile of v1, /device:TPU:1, one launch (start us, length us, event | category | flops | bytes accessed | tf_op | source)
XLA Modules:
  0.0 307.9 jit_solution(2329043552672069988)
XLA Ops:
  0.0 2.7 convolution_convert_fusion.3
  3.8 9.0 %all-to-all-start = ((bf16[8,1,1,512,64]{3,4,2,1,0:T(8,128)(2,1)}), bf16[8,1,1,512,64]{3,4,2,1,0:T(8,128)(2,1)}, u32[]{:S(2)}, u32[]{:S(2)}) async-start(bf16[8,1,1,512,64]{3,4,2,1,0:T(8,128)(2,1)} %broadcast_in_dim.65), calls=%async_computation | async-start | bytes 1048576 | tf_op jit(solution)/shard_map/all_to_all | solution.py:12
  12.9 1.0 copy.59
  13.9 1.9 copy.60
  17.6 2.2 maximum_bitcast_fusion
  19.8 11.1 %all-to-all-done = bf16[8,1,1,512,64]{3,4,2,1,0:T(8,128)(2,1)} async-done(((bf16[8,1,1,512,64]{3,4,2,1,0:T(8,128)(2,1)}), bf16[8,1,1,512,64]{3,4,2,1,0:T(8,128)(2,1)}, u32[]{:S(2)}, u32[]{:S(2)}) %all-to-all-start) | async-done | bytes 524320 | tf_op jit(solution)/shard_map/all_to_all | solution.py:12
  30.9 55.5 %while.17 = (s32[]{:T(128)}, f32[8,1,512]{2,1,0:T(1,128)S(1)}, f32[8,1,512]{2,1,0:T(1,128)S(1)}, f32[8,1,512,64]{2,3,1,0:T(8,128)}, s32[8]{0:T(128)S(1)}, /*inde...) while((s32[]{:T(128)}, f32[8,1,512]{2,1,0:T(1,128)S(1)}, ...), condition=%wide.region_3.4_spmd.clone, body=%wide.region_0.3_spmd.clone.sunk | while | flops 290915840 | bytes 14024361 | solution.py:108
  32.7 3.0 fusion.82
  35.8 1.4 fusion.84
  39.7 3.0 fusion.82
  42.7 1.4 fusion.84
  46.6 3.0 fusion.82
  49.6 1.4 fusion.84
  53.5 3.0 fusion.82
  56.6 1.4 fusion.84
  60.5 3.0 fusion.82
  63.5 1.4 fusion.84
  67.4 3.0 fusion.82
  70.4 1.4 fusion.84
  74.3 3.0 fusion.82
  77.4 1.4 fusion.84
  81.3 3.0 fusion.82
  84.3 1.4 fusion.84
  86.4 9.0 %all_to_all.58 = f32[8,1,512]{2,1,0:T(1,128)S(1)} all-to-all(f32[8,1,512]{2,1,0:T(1,128)S(1)} %get-tuple-element.143), channel_id=1, replica_groups=mesh['seq'=4,'ctx'=8,'head'=8] {'ctx'}, dimensions={0} | all-to-all | bytes 32768 | tf_op jit(solution)/shard_map/all_to_all | solution.py:109
  95.4 9.0 %all_to_all.59 = f32[8,1,512]{2,1,0:T(1,128)S(1)} all-to-all(f32[8,1,512]{2,1,0:T(1,128)S(1)} %get-tuple-element.144), channel_id=1, replica_groups=mesh['seq'=4,'ctx'=8,'head'=8] {'ctx'}, dimensions={0} | all-to-all | bytes 32768 | tf_op jit(solution)/shard_map/all_to_all | solution.py:109
  104.3 4.2 %all-to-all-start.1 = ((f32[8,1,512,64]{2,3,1,0:T(8,128)}), f32[8,1,512,64]{2,3,1,0:T(8,128)}, u32[]{:S(2)}, u32[]{:S(2)}) async-start(f32[8,1,512,64]{2,3,1,0:T(8,128)} %get-tuple-element.142), calls=%async_computation.1 | async-start | bytes 2097152 | tf_op jit(solution)/shard_map/all_to_all | solution.py:109
  111.9 23.9 %all-to-all-done.1 = f32[8,1,512,64]{2,3,1,0:T(8,128)} async-done(((f32[8,1,512,64]{2,3,1,0:T(8,128)}), f32[8,1,512,64]{2,3,1,0:T(8,128)}, u32[]{:S(2)}, u32[]{:S(2)}) %all-to-all-start.1) | async-done | bytes 1048608 | tf_op jit(solution)/shard_map/all_to_all | solution.py:109
  135.8 1.4 multiply_reduce_fusion
  137.4 1.7 convolution_convert_fusion.1
  139.1 1.5 reshape.195
  141.5 5.1 %all-to-all-start.4 = ((bf16[8,64,360]{2,1,0:T(8,128)(2,1)}), bf16[8,64,360]{2,1,0:T(8,128)(2,1)S(1)}, u32[]{:S(2)}, u32[]{:S(2)}) async-start(bf16[8,64,360]{2,1,0:T(8,128)(2,1)} %bitcast.108), calls=%async_computation.4 | async-start | bytes 786432 | tf_op jit(solution)/shard_map/all_to_all | solution.py:33
  146.9 6.3 %all-to-all-done.4 = bf16[8,64,360]{2,1,0:T(8,128)(2,1)S(1)} async-done(((bf16[8,64,360]{2,1,0:T(8,128)(2,1)}), bf16[8,64,360]{2,1,0:T(8,128)(2,1)S(1)}, u32[]{:S(2)}, u32[]{:S(2)}) %all-to-all-start.4) | async-done | bytes 368672 | tf_op jit(solution)/shard_map/all_to_all | solution.py:33
  153.2 1.0 multiply_reduce_fusion.1
  154.9 3.3 %all-to-all-start.5 = ((f32[8,1,64]{2,1,0:T(1,128)}), f32[8,1,64]{2,1,0:T(1,128)S(1)}, u32[]{:S(2)}, u32[]{:S(2)}) async-start(f32[8,1,64]{2,1,0:T(1,128)} %broadcast_in_dim.69), calls=%async_computation.5 | async-start | bytes 8192 | tf_op jit(solution)/shard_map/all_to_all | solution.py:12
  159.1 4.0 %all-to-all-done.5 = f32[8,1,64]{2,1,0:T(1,128)S(1)} async-done(((f32[8,1,64]{2,1,0:T(1,128)}), f32[8,1,64]{2,1,0:T(1,128)S(1)}, u32[]{:S(2)}, u32[]{:S(2)}) %all-to-all-start.5) | async-done | bytes 2080 | tf_op jit(solution)/shard_map/all_to_all | solution.py:12
  163.1 2.0 convolution_convert_fusion.2
  165.1 1.2 copy.71
  166.3 24.1 %all_to_all.60 = bf16[32,16,360]{2,1,0:T(8,128)(2,1)} all-to-all(bf16[32,16,360]{2,1,0:T(8,128)(2,1)S(1)} %bitcast.131), channel_id=1, replica_groups=mesh['seq'=4,'ctx'=8,'head'=8] {'seq','ctx'}, dimensions={0} | all-to-all | bytes 737280 | tf_op jit(solution)/shard_map/all_to_all | solution.py:143
  190.4 1.2 copy.72
  191.7 38.2 %all_to_all.61 = bf16[8,512,360]{1,2,0:T(8,128)(2,1)S(1)} all-to-all(bf16[8,512,360]{1,2,0:T(8,128)(2,1)S(1)} %stack.3), channel_id=1, replica_groups=mesh['seq'=4,'ctx'=8,'head'=8] {'head'}, dimensions={0} | all-to-all | bytes 5898240 | tf_op jit(solution)/shard_map/all_to_all | solution.py:146
  230.0 1.6 copy-done.1
  231.6 2.2 fusion.30
  233.8 7.9 %convolution_convert_fusion = bf16[512,2880]{0,1:T(8,128)(2,1)} fusion(bf16[1,360,2880]{2,1,0:T(8,128)(2,1)} %param.27, bf16[512,2880]{0,1:T(8,128)(2,1)} %bitcast.125, bf16[1,2880,360]{1,2,0:T(8,128)(2,1)} %param.26, f32[512,360]{0,1:T(8,128)} %fusion.30), kind=kOutput, calls=%fused_computation.25 | convolution fusion | flops 2126315520 | bytes 10782720 | tf_op jit(solution)/shard_map/fd,rf->dr/dot_general | solution.py:154
  241.7 38.8 %all_to_all.62 = bf16[8,360,512]{2,1,0:T(8,128)(2,1)} all-to-all(bf16[8,360,512]{2,1,0:T(8,128)(2,1)} %bitcast.126), channel_id=1, replica_groups=mesh['seq'=4,'ctx'=8,'head'=8] {'head'}, dimensions={0} | all-to-all | bytes 5898240 | tf_op jit(solution)/shard_map/all_to_all | solution.py:33
  280.5 2.4 reduce_sum.109
  283.8 7.3 %all-to-all-start.9 = ((bf16[360,32,16]{0,2,1:T(8,128)(2,1)}), bf16[360,32,16]{0,2,1:T(8,128)(2,1)S(1)}, u32[]{:S(2)}, u32[]{:S(2)}) async-start(bf16[360,32,16]{0,2,1:T(8,128)(2,1)} %bitcast.130), calls=%async_computation.9 | async-start | bytes 786432 | tf_op jit(solution)/shard_map/all_to_all | solution.py:160
  291.9 14.1 %all-to-all-done.9 = bf16[360,32,16]{0,2,1:T(8,128)(2,1)S(1)} async-done(((bf16[360,32,16]{0,2,1:T(8,128)(2,1)}), bf16[360,32,16]{0,2,1:T(8,128)(2,1)S(1)}, u32[]{:S(2)}, u32[]{:S(2)}) %all-to-all-start.9) | async-done | bytes 368672 | tf_op jit(solution)/shard_map/all_to_all | solution.py:160
  306.0 1.8 fusion.42
  (89 shorter events, 21.3 us)
Async XLA Ops:
  0.0 137.4 %copy-start = (bf16[512,2880]{0,1:T(8,128)(2,1)S(1)}, bf16[512,2880]{0,1:T(8,128)(2,1)}, u32[]{:S(2)}) copy-start(bf16[512,2880]{0,1:T(8,128)(2,1)} %param.21) | copy-start | bytes 8847364
  0.0 12.9 %copy-start.2 = (bf16[1,2048,1,64]{1,3,2,0:T(8,128)(2,1)S(1)}, bf16[1,2048,1,64]{1,3,2,0:T(8,128)(2,1)}, u32[]{:S(2)}) copy-start(bf16[1,2048,1,64]{1,3,2,0:T(8,128)(2,1)} %param.17) | copy-start | bytes 786436
  0.0 17.6 %copy-start.3 = (bf16[1,64,1,64]{3,1,2,0:T(8,128)(2,1)S(1)}, bf16[1,64,1,64]{3,1,2,0:T(8,128)(2,1)}, u32[]{:S(2)}) copy-start(bf16[1,64,1,64]{3,1,2,0:T(8,128)(2,1)} %param.19) | copy-start | bytes 24580
  0.0 17.6 %copy-start.4 = (bf16[1,64,1,64]{3,1,2,0:T(8,128)(2,1)S(1)}, bf16[1,64,1,64]{3,1,2,0:T(8,128)(2,1)}, u32[]{:S(2)}) copy-start(bf16[1,64,1,64]{3,1,2,0:T(8,128)(2,1)} %param.20) | copy-start | bytes 24580
  3.8 27.1 %all-to-all-start = ((bf16[8,1,1,512,64]{3,4,2,1,0:T(8,128)(2,1)}), bf16[8,1,1,512,64]{3,4,2,1,0:T(8,128)(2,1)}, u32[]{:S(2)}, u32[]{:S(2)}) async-start(bf16[8,1,1,512,64]{3,4,2,1,0:T(8,128)(2,1)} %broadcast_in_dim.65), calls=%async_computation | async-start | bytes 1048576 | tf_op jit(solution)/shard_map/all_to_all | solution.py:12
  104.3 31.4 %all-to-all-start.1 = ((f32[8,1,512,64]{2,3,1,0:T(8,128)}), f32[8,1,512,64]{2,3,1,0:T(8,128)}, u32[]{:S(2)}, u32[]{:S(2)}) async-start(f32[8,1,512,64]{2,3,1,0:T(8,128)} %get-tuple-element.142), calls=%async_computation.1 | async-start | bytes 2097152 | tf_op jit(solution)/shard_map/all_to_all | solution.py:109
  111.0 0.6 copy-start.5
  137.4 9.2 %slice-start = ((s32[32,3]{0,1:T(4,128)}), s32[32,2]{0,1:T(2,128)S(1)}, s32[]{:S(2)}) async-start(s32[32,3]{0,1:T(4,128)} %copy-done.5), calls=%async_computation.10 | async-start | bytes 2048 | tf_op jit(solution)/shard_map/slice.1
  137.4 9.2 %copy-start.6 = (s32[256]{0:T(256)S(1)}, s32[256]{0:T(256)}, u32[]{:S(2)}) copy-start(s32[256]{0:T(256)} %eq.54) | copy-start | bytes 3076
  141.5 11.7 %all-to-all-start.4 = ((bf16[8,64,360]{2,1,0:T(8,128)(2,1)}), bf16[8,64,360]{2,1,0:T(8,128)(2,1)S(1)}, u32[]{:S(2)}, u32[]{:S(2)}) async-start(bf16[8,64,360]{2,1,0:T(8,128)(2,1)} %bitcast.108), calls=%async_computation.4 | async-start | bytes 786432 | tf_op jit(solution)/shard_map/all_to_all | solution.py:33
  154.9 8.2 %all-to-all-start.5 = ((f32[8,1,64]{2,1,0:T(1,128)}), f32[8,1,64]{2,1,0:T(1,128)S(1)}, u32[]{:S(2)}, u32[]{:S(2)}) async-start(f32[8,1,64]{2,1,0:T(1,128)} %broadcast_in_dim.69), calls=%async_computation.5 | async-start | bytes 8192 | tf_op jit(solution)/shard_map/all_to_all | solution.py:12
  191.7 39.9 %copy-start.8 = (bf16[1,2880,360]{1,2,0:T(8,128)(2,1)S(1)}, bf16[1,2880,360]{1,2,0:T(8,128)(2,1)}, u32[]{:S(2)}) copy-start(bf16[1,2880,360]{1,2,0:T(8,128)(2,1)} %param.25) | copy-start | bytes 6220804
  230.0 1.6 copy-start.1
  280.5 10.6 %copy-start.7 = (f32[1,64,4]{1,2,0:T(4,128)S(1)}, f32[1,64,4]{1,2,0:T(4,128)}, u32[]{:S(2)}) copy-start(f32[1,64,4]{1,2,0:T(4,128)} %param.24) | copy-start | bytes 3076
  283.8 22.2 %all-to-all-start.9 = ((bf16[360,32,16]{0,2,1:T(8,128)(2,1)}), bf16[360,32,16]{0,2,1:T(8,128)(2,1)S(1)}, u32[]{:S(2)}, u32[]{:S(2)}) async-start(bf16[360,32,16]{0,2,1:T(8,128)(2,1)} %bitcast.130), calls=%async_computation.9 | async-start | bytes 786432 | tf_op jit(solution)/shard_map/all_to_all | solution.py:160
